TPU v7x, 8 devices: a whole 2x2x1 slice. The times are simulated.
8 devices in a mesh: rep: 2 (over z, y), data: 4 (over x, core).
Axes of the slice: x: 2, y: 2, z: 1, core: 2. Of those that a mesh axis runs over, the one named last changes fastest.
Arguments:
- x_in: bfloat16 [128, 32, 512], P(('rep', 'data'))
- d_out: float32 [128, 32, 512], P(('rep', 'data'))
- weights: bfloat16 [8, 1024, 2048], replicated
- biases: float32 [8, 2048], replicated
Outputs:
- output 1: float32 [8, 1024, 2048], replicated
- output 2: float32 [8, 2048], replicated
- output 3: float32 [128, 32, 512], P(('rep', 'data'))
All inputs are finite; a program needn't handle non-finite values.
Results may differ from a plain program's by a relative error of at most 0.00553299.
Values are sent between devices in bfloat16 or wider.
A program may use at most 1 GiB of HBM per device.

v0:
```python
import jax
import jax.numpy as jnp
from jax import lax
from jax.sharding import PartitionSpec as P


def gate_values(z_all):
    hidden = z_all.shape[-1] // 4
    return (jax.nn.sigmoid(z_all[:, :hidden]), jax.nn.sigmoid(z_all[:, hidden:2 * hidden]),
            jnp.tanh(z_all[:, 2 * hidden:3 * hidden]), jax.nn.sigmoid(z_all[:, 3 * hidden:]))


def layer_forward(x_seq, w_layer, b_layer):
    hidden = x_seq.shape[-1]
    w_rec = w_layer[hidden:]
    x_proj = jnp.einsum('tbh,hg->tbg', x_seq, w_layer[:hidden], preferred_element_type=jnp.float32) + b_layer

    def time_step(carry_in, step_in):
        h_prev, c_prev = carry_in
        z_in, x_t = step_in
        z_all = z_in + jnp.dot(h_prev, w_rec, preferred_element_type=jnp.float32)
        in_g, fg_g, cand_g, out_g = gate_values(z_all)
        c_new = fg_g * c_prev + in_g * cand_g
        h_new = out_g * jnp.tanh(c_new)
        h_low = h_new.astype(jnp.bfloat16)
        y_t = (h_new + x_t.astype(jnp.float32)).astype(jnp.bfloat16)
        return (h_low, c_new), (z_all, c_prev, h_low, y_t)

    batch_rows = x_seq.shape[1]
    init_state = (jnp.zeros((batch_rows, hidden), jnp.bfloat16), jnp.zeros((batch_rows, hidden), jnp.float32))
    _, (z_seq, c_prev_seq, h_seq, y_seq) = lax.scan(time_step, init_state, (x_proj, x_seq))
    return y_seq, z_seq, c_prev_seq, h_seq


def layer_backward(dy_seq, x_seq, w_layer, z_seq, c_prev_seq, h_seq):
    hidden = x_seq.shape[-1]
    w_rec = w_layer[hidden:]

    def time_step(carry_in, step_in):
        dh_rec, dc_next = carry_in
        dy_t, z_all, c_prev = step_in
        in_g, fg_g, cand_g, out_g = gate_values(z_all)
        tanh_c = jnp.tanh(fg_g * c_prev + in_g * cand_g)
        dh_tot = dy_t + dh_rec
        dc_tot = dc_next + dh_tot * out_g * (1.0 - tanh_c * tanh_c)
        dz_all = jnp.concatenate([dc_tot * cand_g * in_g * (1.0 - in_g),
                                  dc_tot * c_prev * fg_g * (1.0 - fg_g),
                                  dc_tot * in_g * (1.0 - cand_g * cand_g),
                                  dh_tot * tanh_c * out_g * (1.0 - out_g)], axis=-1)
        dz_low = dz_all.astype(jnp.bfloat16)
        dh_new = jnp.einsum('bg,hg->bh', dz_low, w_rec, preferred_element_type=jnp.float32)
        return (dh_new, dc_tot * fg_g), (dz_low, jnp.sum(dz_all, axis=0))

    zero_state = jnp.zeros(dy_seq.shape[1:], jnp.float32)
    _, (dz_seq, db_steps) = lax.scan(time_step, (zero_state, zero_state), (dy_seq, z_seq, c_prev_seq), reverse=True)
    dx_seq = dy_seq + jnp.einsum('tbg,hg->tbh', dz_seq, w_layer[:hidden], preferred_element_type=jnp.float32)
    dw_in = jnp.einsum('tbh,tbg->hg', x_seq, dz_seq, preferred_element_type=jnp.float32)
    dw_rec = jnp.einsum('tbh,tbg->hg', h_seq[:-1], dz_seq[1:], preferred_element_type=jnp.float32)
    return dx_seq, jnp.concatenate([dw_in, dw_rec], axis=0), jnp.sum(db_steps, axis=0)


def solution(mesh):
    batch_axes = tuple(mesh.axis_names)

    def device_step(x_in, d_out, weights, biases):
        num_layers = weights.shape[0]
        layer_in = [jnp.swapaxes(x_in, 0, 1)]
        saved_acts = []
        for layer_idx in range(num_layers):
            y_seq, z_seq, c_prev_seq, h_seq = layer_forward(layer_in[layer_idx], weights[layer_idx], biases[layer_idx])
            layer_in.append(y_seq)
            saved_acts.append((z_seq, c_prev_seq, h_seq))
        dy_cur = jnp.swapaxes(d_out, 0, 1)
        dw_parts = []
        db_parts = []
        for layer_idx in range(num_layers - 1, -1, -1):
            z_seq, c_prev_seq, h_seq = saved_acts[layer_idx]
            dy_cur, dw_layer, db_layer = layer_backward(dy_cur, layer_in[layer_idx], weights[layer_idx], z_seq, c_prev_seq, h_seq)
            dw_parts.insert(0, lax.psum(dw_layer, batch_axes))
            db_parts.insert(0, lax.psum(db_layer, batch_axes))
        return jnp.stack(dw_parts), jnp.stack(db_parts), jnp.swapaxes(dy_cur, 0, 1)

    return jax.shard_map(device_step, mesh=mesh,
                         in_specs=(P(batch_axes), P(batch_axes), P(), P()),
                         out_specs=(P(), P(), P(batch_axes)), check_vma=False)
```

profile of v0, /device:TPU:0, one launch (start us, length us, event | category | flops | bytes accessed | tf_op | source)
XLA Modules:
  0.0 3491.0 jit_solution(16464478537638071615)
XLA Ops:
  14.2 11.5 slice_bitcast_fusion
  34.5 127.1 %while.334 = (s32[]{:T(128)}, bf16[16,512]{1,0:T(8,128)(2,1)}, f32[16,512]{1,0:T(8,128)S(1)}, f32[32,16,2048]{2,1,0:T(8,128)}, f32[32,16,512]{2,1,0:T(8,128)}, /...) while((s32[]{:T(128)}, bf16[16,512]{1,0:T(8,128)(2,1)}, ...), condition=%wide.region_1.2_spmd.clone, body=%wide.region_0.1_spmd.clone.sunk | while | flops 33783808 | bytes 2900121 | solution.py:31
  171.2 125.5 %while.335 = (s32[]{:T(128)}, bf16[16,512]{1,0:T(8,128)(2,1)S(1)}, f32[16,512]{1,0:T(8,128)S(1)}, f32[32,16,2048]{2,1,0:T(8,128)}, f32[32,16,512]{2,1,0:T(8,128)...) while((s32[]{:T(128)}, bf16[16,512]{1,0:T(8,128)(2,1)S(1)}, ...), condition=%wide.region_3.4_spmd.clone, body=%wide.region_2.3_spmd.clone.sunk | while | flops 33783808 | bytes 2900121 | solution.py:31
  307.2 125.5 %while.336 = (s32[]{:T(128)}, bf16[16,512]{1,0:T(8,128)(2,1)S(1)}, f32[16,512]{1,0:T(8,128)S(1)}, f32[32,16,2048]{2,1,0:T(8,128)}, f32[32,16,512]{2,1,0:T(8,128)...) while((s32[]{:T(128)}, bf16[16,512]{1,0:T(8,128)(2,1)S(1)}, ...), condition=%wide.region_5.6_spmd.clone, body=%wide.region_4.5_spmd.clone.sunk | while | flops 33783808 | bytes 2900121 | solution.py:31
  443.2 125.5 %while.337 = (s32[]{:T(128)}, bf16[16,512]{1,0:T(8,128)(2,1)S(1)}, f32[16,512]{1,0:T(8,128)S(1)}, f32[32,16,2048]{2,1,0:T(8,128)}, f32[32,16,512]{2,1,0:T(8,128)...) while((s32[]{:T(128)}, bf16[16,512]{1,0:T(8,128)(2,1)S(1)}, ...), condition=%wide.region_7.8_spmd.clone, body=%wide.region_6.7_spmd.clone.sunk | while | flops 33783808 | bytes 2900121 | solution.py:31
  579.0 125.5 %while.338 = (s32[]{:T(128)}, bf16[16,512]{1,0:T(8,128)(2,1)S(1)}, f32[16,512]{1,0:T(8,128)S(1)}, f32[32,16,2048]{2,1,0:T(8,128)}, f32[32,16,512]{2,1,0:T(8,128)...) while((s32[]{:T(128)}, bf16[16,512]{1,0:T(8,128)(2,1)S(1)}, ...), condition=%wide.region_9.10_spmd.clone, body=%wide.region_8.9_spmd.clone.sunk | while | flops 33783808 | bytes 2900121 | solution.py:31
  715.0 133.8 %while.339 = (s32[]{:T(128)}, bf16[16,512]{1,0:T(8,128)(2,1)S(1)}, f32[16,512]{1,0:T(8,128)S(1)}, f32[32,16,2048]{2,1,0:T(8,128)}, f32[32,16,512]{2,1,0:T(8,128)...) while((s32[]{:T(128)}, bf16[16,512]{1,0:T(8,128)(2,1)S(1)}, ...), condition=%wide.region_11.12_spmd.clone, body=%wide.region_10.11_spmd.clone.sunk | while | flops 33783808 | bytes 2900121 | solution.py:31
  859.3 125.6 %while.340 = (s32[]{:T(128)}, bf16[16,512]{1,0:T(8,128)(2,1)S(1)}, f32[16,512]{1,0:T(8,128)S(1)}, f32[32,16,2048]{2,1,0:T(8,128)}, f32[32,16,512]{2,1,0:T(8,128)...) while((s32[]{:T(128)}, bf16[16,512]{1,0:T(8,128)(2,1)S(1)}, ...), condition=%wide.region_13.14_spmd.clone, body=%wide.region_12.13_spmd.clone.sunk | while | flops 33783808 | bytes 2900121 | solution.py:31
  993.8 106.2 %while.341 = (s32[]{:T(128)}, bf16[16,512]{1,0:T(8,128)(2,1)S(1)}, f32[16,512]{1,0:T(8,128)S(1)}, f32[32,16,2048]{2,1,0:T(8,128)}, f32[32,16,512]{2,1,0:T(8,128)...) while((s32[]{:T(128)}, bf16[16,512]{1,0:T(8,128)(2,1)S(1)}, ...), condition=%wide.region_15.16_spmd.clone, body=%wide.region_14.15_spmd.clone.sunk | while | flops 33726464 | bytes 2801797 | solution.py:31
  1101.6 201.4 %while.342 = (s32[]{:T(128)}, f32[16,512]{1,0:T(8,128)S(1)}, f32[16,512]{1,0:T(8,128)}, bf16[32,16,2048]{2,1,0:T(8,128)(2,1)}, f32[32,2048]{1,0:T(8,128)S(1)}, /...) while((s32[]{:T(128)}, f32[16,512]{1,0:T(8,128)S(1)}, ...), condition=%wide.region_18.19_spmd.clone, body=%wide.region_16.18_spmd.clone.sunk | while | flops 34617348 | bytes 3661991 | solution.py:55
  1309.8 182.0 %while.343 = (s32[]{:T(128)}, f32[16,512]{1,0:T(8,128)S(1)}, f32[16,512]{1,0:T(8,128)S(1)}, bf16[32,16,2048]{2,1,0:T(8,128)(2,1)}, f32[32,2048]{1,0:T(8,128)S(1)...) while((s32[]{:T(128)}, f32[16,512]{1,0:T(8,128)S(1)}, ...), condition=%wide.region_21.22_spmd.clone, body=%wide.region_19.21_spmd.clone.sunk | while | flops 34617348 | bytes 3661991 | solution.py:55
  1498.5 182.0 %while.344 = (s32[]{:T(128)}, f32[16,512]{1,0:T(8,128)S(1)}, f32[16,512]{1,0:T(8,128)S(1)}, bf16[32,16,2048]{2,1,0:T(8,128)(2,1)}, f32[32,2048]{1,0:T(8,128)S(1)...) while((s32[]{:T(128)}, f32[16,512]{1,0:T(8,128)S(1)}, ...), condition=%wide.region_24.25_spmd.clone, body=%wide.region_22.24_spmd.clone.sunk | while | flops 34617348 | bytes 3661991 | solution.py:55
  1687.4 182.2 %while.345 = (s32[]{:T(128)}, f32[16,512]{1,0:T(8,128)S(1)}, f32[16,512]{1,0:T(8,128)S(1)}, bf16[32,16,2048]{2,1,0:T(8,128)(2,1)}, f32[32,2048]{1,0:T(8,128)S(1)...) while((s32[]{:T(128)}, f32[16,512]{1,0:T(8,128)S(1)}, ...), condition=%wide.region_27.28_spmd.clone, body=%wide.region_25.27_spmd.clone.sunk | while | flops 34617348 | bytes 3661991 | solution.py:55
  1876.4 182.0 %while.346 = (s32[]{:T(128)}, f32[16,512]{1,0:T(8,128)S(1)}, f32[16,512]{1,0:T(8,128)S(1)}, bf16[32,16,2048]{2,1,0:T(8,128)(2,1)}, f32[32,2048]{1,0:T(8,128)S(1)...) while((s32[]{:T(128)}, f32[16,512]{1,0:T(8,128)S(1)}, ...), condition=%wide.region_30.31_spmd.clone, body=%wide.region_28.30_spmd.clone.sunk | while | flops 34617348 | bytes 3661991 | solution.py:55
  2065.3 182.0 %while.347 = (s32[]{:T(128)}, f32[16,512]{1,0:T(8,128)S(1)}, f32[16,512]{1,0:T(8,128)S(1)}, bf16[32,16,2048]{2,1,0:T(8,128)(2,1)}, f32[32,2048]{1,0:T(8,128)S(1)...) while((s32[]{:T(128)}, f32[16,512]{1,0:T(8,128)S(1)}, ...), condition=%wide.region_33.34_spmd.clone, body=%wide.region_31.33_spmd.clone.sunk | while | flops 34617348 | bytes 3661991 | solution.py:55
  2254.1 182.4 %while.348 = (s32[]{:T(128)}, f32[16,512]{1,0:T(8,128)S(1)}, f32[16,512]{1,0:T(8,128)S(1)}, bf16[32,16,2048]{2,1,0:T(8,128)(2,1)}, f32[32,2048]{1,0:T(8,128)S(1)...) while((s32[]{:T(128)}, f32[16,512]{1,0:T(8,128)S(1)}, ...), condition=%wide.region_36.37_spmd.clone, body=%wide.region_34.36_spmd.clone.sunk | while | flops 34617348 | bytes 3661991 | solution.py:55
  2443.2 131.0 %while.349 = (s32[]{:T(128)}, f32[16,512]{1,0:T(8,128)S(1)}, f32[16,512]{1,0:T(8,128)S(1)}, bf16[32,16,2048]{2,1,0:T(8,128)(2,1)}, f32[32,2048]{1,0:T(8,128)S(1)...) while((s32[]{:T(128)}, f32[16,512]{1,0:T(8,128)S(1)}, ...), condition=%wide.region_39.40_spmd.clone, body=%wide.region_37.39_spmd.clone.sunk | while | flops 34617348 | bytes 3661991 | solution.py:55
  2648.2 10.3 maximum_bitcast_fusion.6
  2658.5 10.2 maximum_bitcast_fusion.4
  2668.7 10.2 maximum_bitcast_fusion.2
  2679.0 10.2 maximum_bitcast_fusion
  2699.1 739.9 %all-reduce.7.cloned.1.call-done = (f32[1,1024,2048]{2,1,0:T(8,128)}, f32[1,1024,2048]{2,1,0:T(8,128)}, f32[1,1024,2048]{2,1,0:T(8,128)}, f32[1,1024,2048]{2,1,0...) async-done(((f32[1,1024,2048]{2,1,0:T(8,128)}, f32[1,1024,2048]{2,1,0:T(8,128)}, ...) | async-done | bytes 67108880 | tf_op jit(solution)/shard_map/psum | solution.py:79
  3439.0 8.0 constant_dynamic-update-slice_fusion.7
  3451.2 8.0 constant_dynamic-update-slice_fusion.5
  (3077 shorter events, 2652.3 us)
Async XLA Ops:
  7.2 2690.4 %all-reduce.5.cloned.1.call-start = ((), (), s32[]{:S(2)}) async-start(), calls=%async_computation | async-start | bytes 131072 | tf_op jit(solution)/shard_map/psum | solution.py:80
  14.2 11.5 copy-start.53
  171.2 125.5 %copy-start.60 = (f32[1,2048]{1,0:T(1,128)S(1)}, f32[1,2048]{1,0:T(1,128)}, u32[]{:S(2)}) copy-start(f32[1,2048]{1,0:T(1,128)} %get-tuple-element.2923) | copy-start | bytes 24580
  307.2 125.5 %copy-start.59 = (f32[1,2048]{1,0:T(1,128)S(1)}, f32[1,2048]{1,0:T(1,128)}, u32[]{:S(2)}) copy-start(f32[1,2048]{1,0:T(1,128)} %get-tuple-element.2922) | copy-start | bytes 24580
  443.2 125.5 %copy-start.58 = (f32[1,2048]{1,0:T(1,128)S(1)}, f32[1,2048]{1,0:T(1,128)}, u32[]{:S(2)}) copy-start(f32[1,2048]{1,0:T(1,128)} %get-tuple-element.2921) | copy-start | bytes 24580
  579.0 125.5 %copy-start.57 = (f32[1,2048]{1,0:T(1,128)S(1)}, f32[1,2048]{1,0:T(1,128)}, u32[]{:S(2)}) copy-start(f32[1,2048]{1,0:T(1,128)} %get-tuple-element.2920) | copy-start | bytes 24580
  715.0 133.8 %copy-start.56 = (f32[1,2048]{1,0:T(1,128)S(1)}, f32[1,2048]{1,0:T(1,128)}, u32[]{:S(2)}) copy-start(f32[1,2048]{1,0:T(1,128)} %get-tuple-element.2926) | copy-start | bytes 24580
  859.3 125.6 %copy-start.55 = (f32[1,2048]{1,0:T(1,128)S(1)}, f32[1,2048]{1,0:T(1,128)}, u32[]{:S(2)}) copy-start(f32[1,2048]{1,0:T(1,128)} %get-tuple-element.2919) | copy-start | bytes 24580
  1101.6 201.4 %copy-start.11 = (f32[16,32,512]{2,1,0:T(8,128)S(1)}, f32[16,32,512]{2,1,0:T(8,128)}, u32[]{:S(2)}) copy-start(f32[16,32,512]{2,1,0:T(8,128)} %param.37) | copy-start | bytes 3145732
  1303.0 6.8 copy-start.52
  1680.6 6.9 copy-start.42
  1680.6 6.9 copy-start.50
  2574.2 13.0 copy-start
  2574.2 13.0 copy-start.41
  2584.0 855.0 %all-reduce.7.cloned.1.call-start = ((), (), s32[]{:S(2)}) async-start(), calls=%async_computation.1 | async-start | bytes 134217728 | tf_op jit(solution)/shard_map/psum | solution.py:79
  2658.5 10.2 copy-start.8
  2668.7 10.2 copy-start.9
  3439.0 8.0 copy-start.10
  3447.0 12.2 slice-start.6
  3451.2 8.0 slice-start.7
  3451.2 12.2 slice-start.4
  3463.4 12.2 slice-start.2
  3467.6 8.0 slice-start.3
  3467.6 12.2 slice-start
  (47 other events, 199.0 us)
Sparse Core Ops, SparseCore 0:
  2584.1 46.5 all-reduce.4
  2689.3 749.6 all-reduce.6
where the time goes:
time: 3550 us; the launch traced here: 3490 us
  matrix products  1310 us (37%)
  other arithmetic  999 us (28%)
  waiting for transfers between devices  740 us (21%)
  local copies, waits for them, and re-layouts  415 us (12%)
    psum x1, waiting for transfers between devices, device_step(): dw_parts.insert(0, lax.psum(dw_layer, batch_axes))  740 us
    dot_general x256, matrix products, time_step(): z_all = z_in + jnp.dot(h_prev, w_rec, preferred_element_type=jnp.float32)  653 us
    dot_general x256, matrix products, time_step(): jnp.einsum('bg,hg->bh', dz_low, w_rec, preferred_element_type=jnp.float32)  522 us
    concatenate x512, other arithmetic, time_step(): jnp.concatenate([dc_tot * cand_g * in_g * (1.0 - in_g), dc_tot * c_prev *...  448 us
    dynamic_update_slice x736, other arithmetic, layer_forward(): lax.scan(time_step, init_state, (x_proj, x_seq))  332 us
    squeeze x256, local copies, waits for them, and re-layouts, layer_forward(): lax.scan(time_step, init_state, (x_proj, x_seq))  234 us
    dynamic_update_slice x256, other arithmetic, layer_backward(): lax.scan(time_step, (zero_state, zero_state), (dy_seq, z_seq, c_prev_seq)...  162 us
  transfers between devices with their start and end apart: 2, of which 1 were waited for; matrix products, arithmetic and copies ran while one was open for 3% of the time, Pallas kernels for 0%

commit v1 on v0

v1 whole, which is shorter than its diff:
```python
import functools

import jax
import jax.numpy as jnp
from jax import lax
from jax.experimental import pallas as pl
from jax.experimental.pallas import tpu as pltpu
from jax.sharding import PartitionSpec as P

HID = 512
GATES = 4 * HID
ROWS = 128
OWN = 16
STEPS = 32
PIECE = 4
PIECES = STEPS // PIECE
COL = 256
RING = 4
F32 = jnp.float32
BF16 = jnp.bfloat16
MESH = pl.DeviceIdType.MESH


def dot(a, b):
    return jnp.dot(a, b, preferred_element_type=F32)


def pipeline_kernel(n_data, x_hbm, dout_hbm, w_hbm, b_hbm,
                    dw_hbm, db_ref, dx_hbm, gates_hbm,
                    w, wt, bias, x_buf, h_buf, c_buf, dy_buf, dw_acc, db_acc, xh_t, dz, dr, dc, y_out, g_out, g_in, dx_out,
                    x_sem, xin_sem, xin_send, y_send, g_wsem, g_rsem, dy_sem, din_sem, din_send, dx_send, dxs_send, dx_recv,
                    load_sem):
    layer = lax.axis_index('rep') * n_data + lax.axis_index('data')
    first, last = layer == 0, layer == 7

    def place(idx):
        return {'rep': idx // n_data, 'data': lax.rem(idx, n_data)}

    my_rows = pl.ds(pl.multiple_of(layer * OWN, OWN), OWN)

    w_copy = pltpu.make_async_copy(w_hbm.at[layer], w, load_sem.at[0])
    b_copy = pltpu.make_async_copy(b_hbm.at[layer], bias, load_sem.at[1])
    w_copy.start()
    b_copy.start()

    def x_piece(p, remote):
        src, dst = x_hbm.at[pl.ds(p * PIECE, PIECE)], x_buf.at[pl.ds(p * PIECE, PIECE), my_rows]
        if remote:
            return pltpu.make_async_remote_copy(src, dst, xin_send.at[p], xin_sem.at[p], device_id=place(0), device_id_type=MESH)
        return pltpu.make_async_copy(src, dst, xin_sem.at[p])

    def d_piece(p, remote):
        src, dst = dout_hbm.at[pl.ds(p * PIECE, PIECE)], dy_buf.at[pl.ds(p * PIECE, PIECE), my_rows]
        if remote:
            return pltpu.make_async_remote_copy(src, dst, din_send.at[p], din_sem.at[p], device_id=place(7), device_id_type=MESH)
        return pltpu.make_async_copy(src, dst, din_sem.at[p])

    @pl.when(first)
    def _():
        for p in range(PIECES):
            x_piece(p, False).start()

    @pl.when(jnp.logical_not(first))
    def _():
        for p in range(PIECES):
            x_piece(p, True).start()

    @pl.when(last)
    def _():
        for p in range(PIECES):
            d_piece(p, False).start()

    @pl.when(jnp.logical_not(last))
    def _():
        for p in reversed(range(PIECES // 2, PIECES)):
            d_piece(p, True).start()

    h_buf[0] = jnp.zeros((ROWS, HID), BF16)
    c_buf[0] = jnp.zeros((ROWS, HID), F32)
    w_copy.wait()
    b_copy.wait()

    def make_wt():
        for r in range(4):
            def body(n, carry):
                col = pl.multiple_of(n * COL, COL)
                wt[pl.ds(col, COL), r * COL:(r + 1) * COL] = w[r * COL:(r + 1) * COL, pl.ds(col, COL)].T
                return carry
            lax.fori_loop(0, GATES // COL, body, 0)

    @pl.when(jnp.logical_not(first))
    def _():
        make_wt()

    def y_copy(t, slot):
        return pltpu.make_async_remote_copy(y_out.at[slot], x_buf.at[t], y_send.at[slot], x_sem.at[t],
                                            device_id=place(lax.min(layer + 1, 7)), device_id_type=MESH)

    def g_write(t, slot):
        return pltpu.make_async_copy(g_out.at[slot], gates_hbm.at[t], g_wsem.at[slot])

    def fwd_step(t, carry):
        slot = lax.rem(t, RING)
        gslot = lax.rem(t, 2)

        @pl.when(jnp.logical_and(first, lax.rem(t, PIECE) == 0))
        def _():
            p = t // PIECE
            pltpu.make_async_copy(x_buf.at[pl.ds(p * PIECE, PIECE)], x_buf.at[pl.ds(p * PIECE, PIECE)], xin_sem.at[p]).wait()

        @pl.when(jnp.logical_not(first))
        def _():
            y_copy(t, slot).wait_recv()

        @pl.when(t >= 2)
        def _():
            g_write(t - 2, gslot).wait()

        @pl.when(jnp.logical_and(jnp.logical_not(last), t >= RING))
        def _():
            y_copy(t - RING, slot).wait_send()

        for j in range(HID // COL):
            hc = slice(j * COL, (j + 1) * COL)
            z = []
            for q in range(4):
                cols = slice(q * HID + j * COL, q * HID + (j + 1) * COL)
                z.append(dot(x_buf[t], w[:HID, cols]) + dot(h_buf[t], w[HID:, cols]) + bias[:, cols])
            in_g, fg_g, cand_g, out_g = jax.nn.sigmoid(z[0]), jax.nn.sigmoid(z[1]), jnp.tanh(z[2]), jax.nn.sigmoid(z[3])
            for q, gate in enumerate((in_g, fg_g, cand_g, out_g)):
                g_out[gslot, :, q * HID + j * COL:q * HID + (j + 1) * COL] = gate
            c_new = fg_g * c_buf[t, :, hc] + in_g * cand_g
            h_new = out_g * jnp.tanh(c_new)
            c_buf[t + 1, :, hc] = c_new
            h_buf[t + 1, :, hc] = h_new.astype(BF16)
            y_out[slot, :, hc] = (h_new + x_buf[t, :, hc].astype(F32)).astype(BF16)

        g_write(t, gslot).start()

        @pl.when(jnp.logical_not(last))
        def _():
            y_copy(t, slot).start()
        return carry

    lax.fori_loop(0, STEPS, fwd_step, 0)

    @pl.when(jnp.logical_not(last))
    def _():
        for p in reversed(range(PIECES // 2)):
            d_piece(p, True).start()

    @pl.when(first)
    def _():
        make_wt()

    g_write(STEPS - 2, 0).wait()
    g_write(STEPS - 1, 1).wait()

    def g_read(t, slot):
        return pltpu.make_async_copy(gates_hbm.at[t], g_in.at[slot], g_rsem.at[slot])

    def dy_copy(t, slot):
        return pltpu.make_async_remote_copy(dx_out.at[slot], dy_buf.at[t], dx_send.at[slot], dy_sem.at[t],
                                            device_id=place(lax.max(layer - 1, 0)), device_id_type=MESH)

    def home_copy(t, slot, dev):
        return pltpu.make_async_remote_copy(dx_out.at[slot, dev * OWN:(dev + 1) * OWN], dx_hbm.at[t], dxs_send.at[slot, dev], dx_recv.at[t],
                                            device_id=place(dev), device_id_type=MESH)

    def own_copy(t, slot):
        return pltpu.make_async_copy(dx_out.at[slot, :OWN], dx_hbm.at[t], dxs_send.at[slot, 0])

    g_read(STEPS - 1, 1).start()
    g_read(STEPS - 2, 0).start()
    dr[...] = jnp.zeros((ROWS, HID), F32)
    dc[...] = jnp.zeros((ROWS, HID), F32)
    db_acc[...] = jnp.zeros((8, GATES), F32)
    dw_acc[...] = jnp.zeros((2 * HID, GATES), F32)

    def bwd_step(t, half):
        slot = lax.rem(t, RING)

        @pl.when(jnp.logical_and(last, lax.rem(t, PIECE) == PIECE - 1))
        def _():
            p = t // PIECE
            pltpu.make_async_copy(dy_buf.at[pl.ds(p * PIECE, PIECE)], dy_buf.at[pl.ds(p * PIECE, PIECE)], din_sem.at[p]).wait()

        @pl.when(jnp.logical_not(last))
        def _():
            dy_copy(t, slot).wait_recv()

        g_read(t, half).wait()

        for j in range(HID // COL):
            hc = slice(j * COL, (j + 1) * COL)
            in_g, fg_g, cand_g, out_g = (g_in[half, :, q * HID + j * COL:q * HID + (j + 1) * COL] for q in range(4))
            tanh_c = jnp.tanh(c_buf[t + 1, :, hc])
            dh_tot = dy_buf[t, :, hc] + dr[:, hc]
            dc_tot = dc[:, hc] + dh_tot * out_g * (1.0 - tanh_c * tanh_c)
            parts = (dc_tot * cand_g * in_g * (1.0 - in_g),
                     dc_tot * c_buf[t, :, hc] * fg_g * (1.0 - fg_g),
                     dc_tot * in_g * (1.0 - cand_g * cand_g),
                     dh_tot * tanh_c * out_g * (1.0 - out_g))
            dc[:, hc] = dc_tot * fg_g
            for q, part in enumerate(parts):
                cols = slice(q * HID + j * COL, q * HID + (j + 1) * COL)
                dz[half, :, cols] = part.astype(BF16)
                db_acc[:, cols] += jnp.sum(part.reshape(ROWS // 8, 8, COL), axis=0)

        @pl.when(t >= 2)
        def _():
            g_read(t - 2, half).start()

        @pl.when(jnp.logical_and(jnp.logical_not(first), t < STEPS - RING))
        def _():
            dy_copy(t + RING, slot).wait_send()

        @pl.when(jnp.logical_and(first, t < STEPS - RING))
        def _():
            own_copy(t + RING, slot).wait()
            for dev in range(1, 8):
                home_copy(t + RING, slot, dev).wait_send()

        dr[...] = dot(dz[half], wt[:, HID:])
        dx_out[slot] = dy_buf[t] + dot(dz[half], wt[:, :HID])

        @pl.when(jnp.logical_not(first))
        def _():
            dy_copy(t, slot).start()

        @pl.when(first)
        def _():
            own_copy(t, slot).start()
            for dev in range(1, 8):
                home_copy(t, slot, dev).start()

    def bwd_pair(k, carry):
        t0 = STEPS - 2 - 2 * k
        xh_t[:HID] = x_buf[pl.ds(t0, 2)].reshape(2 * ROWS, HID).T
        xh_t[HID:] = h_buf[pl.ds(t0, 2)].reshape(2 * ROWS, HID).T
        bwd_step(t0 + 1, 1)
        bwd_step(t0, 0)
        def block(n, c):
            cols = pl.ds(pl.multiple_of(n * COL, COL), COL)
            dw_acc[:, cols] += dot(xh_t[...], dz[:, :, cols].reshape(2 * ROWS, COL))
            return c
        lax.fori_loop(0, GATES // COL, block, 0)
        return carry

    lax.fori_loop(0, STEPS // 2, bwd_pair, 0)

    dw_copy = pltpu.make_async_copy(dw_acc, dw_hbm.at[0], load_sem.at[0])
    dw_copy.start()
    db_ref[...] = jnp.sum(db_acc[...], axis=0, keepdims=True)

    @pl.when(jnp.logical_not(last))
    def _():
        for s in range(RING):
            y_copy(STEPS - RING + s, s).wait_send()
        for p in range(PIECES):
            d_piece(p, True).wait_send()

    @pl.when(jnp.logical_not(first))
    def _():
        for s in range(RING):
            dy_copy(s, s).wait_send()
        for p in range(PIECES):
            x_piece(p, True).wait_send()
        for t in range(STEPS):
            home_copy(t, 0, 0).wait_recv()

    @pl.when(first)
    def _():
        for s in range(RING):
            own_copy(s, s).wait()
            for dev in range(1, 8):
                home_copy(s, s, dev).wait_send()

    dw_copy.wait()


def solution(mesh):
    batch_axes = tuple(mesh.axis_names)
    n_data = mesh.shape['data']

    def device_step(x_in, d_out, weights, biases):
        x_seq = jnp.swapaxes(x_in, 0, 1)
        d_seq = jnp.swapaxes(d_out, 0, 1)
        hbm = pl.BlockSpec(memory_space=pl.ANY)
        dma = pltpu.SemaphoreType.DMA
        dw, db, dx, _ = pl.pallas_call(
            functools.partial(pipeline_kernel, n_data),
            out_shape=(jax.ShapeDtypeStruct((1, 2 * HID, GATES), F32),
                       jax.ShapeDtypeStruct((1, GATES), F32),
                       jax.ShapeDtypeStruct((STEPS, OWN, HID), F32),
                       jax.ShapeDtypeStruct((STEPS, ROWS, GATES), F32)),
            in_specs=[hbm] * 4,
            out_specs=(hbm, pl.BlockSpec(memory_space=pltpu.VMEM), hbm, hbm),
            scratch_shapes=[
                pltpu.VMEM((2 * HID, GATES), BF16),
                pltpu.VMEM((GATES, 2 * HID), BF16),
                pltpu.VMEM((1, GATES), F32),
                pltpu.VMEM((STEPS, ROWS, HID), BF16),
                pltpu.VMEM((STEPS + 1, ROWS, HID), BF16),
                pltpu.VMEM((STEPS + 1, ROWS, HID), F32),
                pltpu.VMEM((STEPS, ROWS, HID), F32),
                pltpu.VMEM((2 * HID, GATES), F32),
                pltpu.VMEM((8, GATES), F32),
                pltpu.VMEM((2 * HID, 2 * ROWS), BF16),
                pltpu.VMEM((2, ROWS, GATES), BF16),
                pltpu.VMEM((ROWS, HID), F32),
                pltpu.VMEM((ROWS, HID), F32),
                pltpu.VMEM((RING, ROWS, HID), BF16),
                pltpu.VMEM((2, ROWS, GATES), F32),
                pltpu.VMEM((2, ROWS, GATES), F32),
                pltpu.VMEM((RING, ROWS, HID), F32),
                dma((STEPS,)), dma((PIECES,)), dma((PIECES,)), dma((RING,)), dma((2,)), dma((2,)),
                dma((STEPS,)), dma((PIECES,)), dma((PIECES,)), dma((RING,)), dma((RING, 8)), dma((STEPS,)),
                dma((2,)),
            ],
            compiler_params=pltpu.CompilerParams(has_side_effects=True, vmem_limit_bytes=66000000),
        )(x_seq, d_seq, weights, biases.reshape(8, 1, GATES))
        dw_all = lax.all_gather(dw, batch_axes, axis=0, tiled=True)
        db_all = lax.all_gather(db, batch_axes, axis=0, tiled=True)
        return dw_all, db_all, jnp.swapaxes(dx, 0, 1)

    return jax.shard_map(device_step, mesh=mesh,
                         in_specs=(P(batch_axes), P(batch_axes), P(), P()),
                         out_specs=(P(), P(), P(batch_axes)), check_vma=False)
```

time: 3550 us -> 583 us (0.16); the launches traced: 3490 us -> 582 us
  matrix products: 1310 us -> 0 us
  other arithmetic: 999 us -> 0 us
  waiting for transfers between devices: 740 us -> 282 us
  local copies, waits for them, and re-layouts: 415 us -> 53.7 us
  Pallas kernels: 0 us -> 222 us
    dot_general x544 -> x0, matrix products: 1310 us -> none  [the longest x256 653 us: time_step(): z_all = z_in + jnp.dot(h_prev, w_rec, preferred_element_type=jnp.float32)]
    psum x2 -> x0, waiting for transfers between devices: 740 us -> none  [the longest x1 740 us: device_step(): dw_parts.insert(0, lax.psum(dw_layer, batch_axes))]
    dynamic_update_slice x992 -> x0, other arithmetic: 494 us -> none  [the longest x736 332 us: layer_forward(): lax.scan(time_step, init_state, (x_proj, x_seq))]
    concatenate x512 -> x0, other arithmetic: 448 us -> none  [time_step(): jnp.concatenate([dc_tot * cand_g * in_g * (1.0 - in_g), dc_tot * c_prev *...]
    all_gather x0 -> x1, waiting for transfers between devices: none -> 281 us  [device_step(): dw_all = lax.all_gather(dw, batch_axes, axis=0, tiled=True)]
    squeeze x256 -> x0, local copies, waits for them, and re-layouts: 234 us -> none  [layer_forward(): lax.scan(time_step, init_state, (x_proj, x_seq))]
    pallas_call x0 -> x1, Pallas kernels: none -> 222 us  [device_step(): pl.pallas_call(functools.partial(pipeline_kernel, n_data), out_shape=(jax...]
    another operation x57 -> x0, local copies, waits for them, and re-layouts: 57.2 us -> none
  transfers between devices with their start and end apart: 2 -> 1, of which waited for: 1 -> 1; matrix products, arithmetic and copies ran while one was open for 3% -> 1% of each run, Pallas kernels for 0% -> 0%
where the time goes in v1:
time: 583 us; the launch traced here: 582 us
  waiting for transfers between devices  282 us (48%)
  Pallas kernels  222 us (38%)
  local copies, waits for them, and re-layouts  53.7 us (9%)
  between operations  14 us (2%)
  blocking collectives  11 us (2%)
    all_gather x1, waiting for transfers between devices, device_step(): dw_all = lax.all_gather(dw, batch_axes, axis=0, tiled=True)  281 us
    pallas_call x1, Pallas kernels, device_step(): pl.pallas_call(functools.partial(pipeline_kernel, n_data), out_shape=(jax...  222 us
    unnamed x5, local copies, waits for them, and re-layouts  52.2 us
  transfers between devices with their start and end apart: 1, of which 1 were waited for; matrix products, arithmetic and copies ran while one was open for 1% of the time, Pallas kernels for 0%

profile of v1, /device:TPU:0, one launch (start us, length us, event | category | flops | bytes accessed | tf_op | source)
XLA Modules:
  0.0 582.4 jit_solution(2982153814918298104)
XLA Ops:
  7.2 0.0 all-gather.3.cloned.1.call-start
  7.2 1.5 reshape.9.b_hbm
  8.7 2.1 copy.18
  10.9 2.8 copy.17
  13.7 222.1 %shard_map.67 = (f32[1,1024,2048]{2,1,0:T(8,128)}, f32[1,2048]{1,0:T(1,128)}, f32[32,16,512]{2,1,0:T(8,128)}, f32[32,128,2048]{2,1,0:T(8,128)}) custom-call(bf16[32,16,512]{2,1,0:T(8,128)(2,1)} %bitcast.12, f32[32,16,512]{2,1,0:T(8,128)} %bitcast.11, bf16[8,1024,2048]{2,1,0:T(8,128)(2,1)} %w_hbm.1, f32[8,1,2048]{2,1,0:T(1,128)} %reshape.9.b_hbm), custom_call_target="tpu_custom_call" | custom-call | tf_op jit(solution)/shard_map/pallas_call | solution.py:291
  235.8 0.0 all-gather.3.cloned.1.call-update
  235.8 11.0 %all-gather = f32[8,1,2048]{2,1,0:T(1,128)S(1)} all-gather(f32[1,1,2048]{2,1,0:T(1,128)} %bitcast.15), channel_id=1, replica_groups=mesh['rep'=2,'data'=4] {'rep','data'}, dimensions={0}, use_global_device_ids=true | all-gather | bytes 73728 | tf_op jit(solution)/shard_map/all_gather | solution.py:324
  246.8 0.7 copy.19
  247.5 2.8 copy.12
  250.3 281.5 %all-gather.3.cloned.1.call-done = f32[8,1024,2048]{2,1,0:T(8,128)} async-done(((f32[1,1024,2048]{2,1,0:T(8,128)}), f32[8,1024,2048]{2,1,0:T(8,128)}) %all-gather.3.cloned.1.call-update) | async-done | bytes 67108880 | tf_op jit(solution)/shard_map/all_gather | solution.py:323
  531.8 43.8 %copy.21 = f32[8,1024,2048]{2,1,0:T(8,128)} copy(f32[8,1024,2048]{2,1,0:T(8,128)} %all-gather.3.cloned.1.call-done) | data formatting | bytes 134217728
Async XLA Ops:
  7.2 524.6 %all-gather.3.cloned.1.call-start = ((), (), s32[]{:S(2)}) async-start(), calls=%async_computation | async-start | bytes 75497472 | tf_op jit(solution)/shard_map/all_gather | solution.py:323
Sparse Core Ops, SparseCore 0:
  235.9 295.8 all-gather.2

commit v2 on v0

v2 whole, which is shorter than its diff:
```python
import functools

import jax
import jax.numpy as jnp
from jax import lax
from jax.experimental import pallas as pl
from jax.experimental.pallas import tpu as pltpu
from jax.sharding import PartitionSpec as P

HID = 512
GATES = 4 * HID
ROWS = 128
OWN = 16
STEPS = 32
LOCAL = 4
CHIPS = 4
PIECE = 4
PIECES = STEPS // PIECE
COL = 256
KT = 2 * HID // COL
NT = GATES // COL
REC = 5 * HID
RING = 4
F32 = jnp.float32
BF16 = jnp.bfloat16
MESH = pl.DeviceIdType.MESH


def dot(a, b):
    return jnp.dot(a, b, preferred_element_type=F32)


def sum_dots(pairs):
    total = None
    for a, b in pairs:
        part = dot(a, b)
        total = part if total is None else total + part
    return total


def recurrence_kernel(n_data, x_hbm, dout_hbm, w_hbm, bias,
                      xh_hbm, dz_hbm, dx_hbm, db_hbm, rec_hbm,
                      w, x_buf, dy_buf, lhs, hn, xn, cs, rec, y_out, dz, dyn, dr, dc, dx_out, db_acc, db_sum,
                      w_sem, x_sem, xin_sem, xin_send, y_send, lhs_sem, rec_wsem, rec_rsem, dy_sem, din_sem, din_send,
                      dz_sem, dx_send, home_sem, dx_recv, db_sem):
    rep, data = lax.axis_index('rep'), lax.axis_index('data')
    core = lax.rem(data, 2)
    chip = rep * (n_data // 2) + data // 2
    me = 2 * chip + core
    first, second = core == 0, core == 1
    partner = {'rep': rep, 'data': data + 1 - 2 * core}
    my_rows = pl.ds(pl.multiple_of(me * OWN, OWN), OWN)

    def place(dev):
        return {'rep': dev // n_data, 'data': dev % n_data}

    def w_copy(l, k, n):
        return pltpu.make_async_copy(w_hbm.at[core * LOCAL + l, pl.ds(k * COL, COL), pl.ds(n * COL, COL)], w.at[l, k, n], w_sem.at[l])

    def x_piece(p, dev, remote):
        src, dst = x_hbm.at[pl.ds(p * PIECE, PIECE)], x_buf.at[pl.ds(p * PIECE, PIECE), my_rows]
        if remote:
            return pltpu.make_async_remote_copy(src, dst, xin_send.at[p, dev // 2], xin_sem.at[p], device_id=place(dev), device_id_type=MESH)
        return pltpu.make_async_copy(src, dst, xin_sem.at[p])

    def d_piece(p, dev, remote):
        src, dst = dout_hbm.at[pl.ds(p * PIECE, PIECE)], dy_buf.at[pl.ds(p * PIECE, PIECE), my_rows]
        if remote:
            return pltpu.make_async_remote_copy(src, dst, din_send.at[p, dev // 2], din_sem.at[p], device_id=place(dev), device_id_type=MESH)
        return pltpu.make_async_copy(src, dst, din_sem.at[p])

    def gather(piece, p, which):
        for dev in range(which, 2 * CHIPS, 2):
            @pl.when(me == dev)
            def _():
                piece(p, dev, False).start()

            @pl.when(me != dev)
            def _():
                piece(p, dev, True).start()

    def gathered(piece, p, which):
        for dev in range(which, 2 * CHIPS, 2):
            @pl.when(me != dev)
            def _():
                piece(p, dev, True).wait_send()

    for p in range(PIECES):
        gather(x_piece, p, 0)
    for l in range(LOCAL):
        for k in range(KT):
            for n in range(NT):
                w_copy(l, k, n).start()
    for p in reversed(range(PIECES)):
        gather(d_piece, p, 1)

    for l in range(LOCAL):
        hn[l][...] = jnp.zeros((ROWS, HID), BF16)
        cs[l][...] = jnp.zeros((ROWS, HID), F32)
    for l in range(LOCAL):
        for k in range(KT):
            for n in range(NT):
                w_copy(l, k, n).wait()

    def y_copy(t, slot):
        return pltpu.make_async_remote_copy(y_out.at[slot], x_buf.at[t], y_send.at[slot], x_sem.at[t], device_id=partner, device_id_type=MESH)

    def lhs_write(l, t, slot):
        return pltpu.make_async_copy(lhs[l].at[slot], xh_hbm.at[l, t], lhs_sem.at[l, slot])

    def rec_write(l, t, slot):
        return pltpu.make_async_copy(rec[l].at[slot], rec_hbm.at[l, t], rec_wsem.at[l, slot])

    def guard(cond):
        if isinstance(cond, bool):
            return (lambda f: f()) if cond else (lambda f: None)
        return pl.when(cond)

    def valid(t, full):
        return True if full else jnp.logical_and(t >= 0, t < STEPS)

    def both(a, b):
        return b if a is True else jnp.logical_and(a, b)

    def fwd_cell(l, t, slot):
        for j in range(HID // COL):
            hc = slice(j * COL, (j + 1) * COL)
            z = []
            for q in range(4):
                n = q * (HID // COL) + j
                z.append(sum_dots([(lhs[l][slot, :, k * COL:(k + 1) * COL], w[l, k, n]) for k in range(KT)])
                         + bias[pl.ds(core * LOCAL + l, 1), n * COL:(n + 1) * COL])
            in_g, fg_g, cand_g, out_g = jax.nn.sigmoid(z[0]), jax.nn.sigmoid(z[1]), jnp.tanh(z[2]), jax.nn.sigmoid(z[3])
            c_prev = cs[l][:, hc]
            for q, value in enumerate((in_g, fg_g, cand_g, out_g, c_prev)):
                rec[l][slot, :, q * HID + j * COL:q * HID + (j + 1) * COL] = value
            c_new = fg_g * c_prev + in_g * cand_g
            h_new = out_g * jnp.tanh(c_new)
            cs[l][:, hc] = c_new
            hn[l][:, hc] = h_new.astype(BF16)
            y_new = (h_new + lhs[l][slot, :, hc].astype(F32)).astype(BF16)
            if l < LOCAL - 1:
                xn[l][:, hc] = y_new
            else:
                y_out[lax.rem(t, RING), :, hc] = y_new

    def fwd_wave(s, full):
        t_of = [s - l for l in range(LOCAL)]
        slot_of = [lax.rem(t + RING, 2) for t in t_of]

        @pl.when(jnp.logical_and(first, both(valid(s, full), lax.rem(s, PIECE) == 0)))
        def _():
            p = s // PIECE
            pltpu.make_async_copy(x_buf.at[pl.ds(p * PIECE, PIECE)], x_buf.at[pl.ds(p * PIECE, PIECE)], xin_sem.at[p]).wait()

        @pl.when(both(valid(s, full), second))
        def _():
            y_copy(s, 0).wait_recv()

        for l in range(LOCAL):
            t, slot = t_of[l], slot_of[l]

            @guard(True if full else jnp.logical_and(t >= 2, t < STEPS))
            def _():
                lhs_write(l, t - 2, slot).wait()
                rec_write(l, t - 2, slot).wait()

        t_top = t_of[LOCAL - 1]

        @pl.when(jnp.logical_and(first, jnp.logical_and(t_top >= RING, t_top < STEPS)))
        def _():
            y_copy(t_top - RING, lax.rem(t_top, RING)).wait_send()

        def assemble(l):
            lhs[l][slot_of[l], :, :HID] = x_buf[t_of[0]] if l == 0 else xn[l - 1][...]
            lhs[l][slot_of[l], :, HID:] = hn[l][...]

        if full:
            for l in range(LOCAL):
                assemble(l)
            for l in range(LOCAL):
                fwd_cell(l, t_of[l], slot_of[l])
        else:
            for l in reversed(range(LOCAL)):
                @pl.when(valid(t_of[l], False))
                def _():
                    assemble(l)
                    fwd_cell(l, t_of[l], slot_of[l])

        for l in range(LOCAL):
            t, slot = t_of[l], slot_of[l]

            @guard(valid(t, full))
            def _():
                lhs_write(l, t, slot).start()

            @pl.when(both(valid(t, full), t < STEPS - 2))
            def _():
                rec_write(l, t, slot).start()

        @pl.when(both(valid(t_top, full), first))
        def _():
            y_copy(t_top, lax.rem(t_top, RING)).start()

    def run_waves(wave, lo, hi, full):
        def body(s, carry):
            wave(s, full)
            return carry
        lax.fori_loop(lo, hi, body, 0)

    run_waves(fwd_wave, 0, LOCAL + 1, False)
    run_waves(fwd_wave, LOCAL + 1, STEPS, True)
    run_waves(fwd_wave, STEPS, STEPS + LOCAL - 1, False)

    def turn(i, carry):
        k, n = i // NT, lax.rem(i, NT)
        for l0 in range(0, LOCAL, 2):
            tiles = [w[l, k, n].T for l in (l0, l0 + 1)]
            for l, tile in zip((l0, l0 + 1), tiles):
                w[l, k, n] = tile
        return carry

    lax.fori_loop(0, KT * NT, turn, 0)

    for l in range(LOCAL):
        for slot in range(2):
            lhs_write(l, STEPS - 2 + slot, slot).wait()

    def rec_read(l, t, slot):
        return pltpu.make_async_copy(rec_hbm.at[l, t], rec[l].at[slot], rec_rsem.at[l, slot])

    def dz_write(l, t, slot):
        return pltpu.make_async_copy(dz[l].at[slot], dz_hbm.at[l, t], dz_sem.at[l, slot])

    def dy_copy(t, slot):
        return pltpu.make_async_remote_copy(dx_out.at[slot], dy_buf.at[t], dx_send.at[slot], dy_sem.at[t], device_id=partner, device_id_type=MESH)

    def home_copy(t, slot):
        rows = pl.ds(pl.multiple_of((2 * chip + 1) * OWN, OWN), OWN)
        return pltpu.make_async_remote_copy(dx_out.at[slot, rows], dx_hbm.at[t], dx_send.at[slot], dx_recv.at[t], device_id=partner, device_id_type=MESH)

    def own_copy(t, slot):
        return pltpu.make_async_copy(dx_out.at[slot, my_rows], dx_hbm.at[t], home_sem.at[slot])

    for l in range(LOCAL):
        dr[l][...] = jnp.zeros((ROWS, HID), F32)
        dc[l][...] = jnp.zeros((ROWS, HID), F32)
    db_acc[...] = jnp.zeros((LOCAL, 8, GATES), F32)

    def bwd_cell(l, t, slot):
        out_slot = lax.rem(t, RING)
        for j in range(HID // COL):
            hc = slice(j * COL, (j + 1) * COL)
            in_g, fg_g, cand_g, out_g, c_prev = (rec[l][slot, :, q * HID + j * COL:q * HID + (j + 1) * COL] for q in range(5))
            tanh_c = jnp.tanh(fg_g * c_prev + in_g * cand_g)
            dy = dy_buf[t, :, hc] if l == LOCAL - 1 else dyn[l][:, hc]
            dh_tot = dy + dr[l][:, hc]
            dc_tot = dc[l][:, hc] + dh_tot * out_g * (1.0 - tanh_c * tanh_c)
            parts = (dc_tot * cand_g * in_g * (1.0 - in_g),
                     dc_tot * c_prev * fg_g * (1.0 - fg_g),
                     dc_tot * in_g * (1.0 - cand_g * cand_g),
                     dh_tot * tanh_c * out_g * (1.0 - out_g))
            dc[l][:, hc] = dc_tot * fg_g
            for q, part in enumerate(parts):
                cols = slice(q * HID + j * COL, q * HID + (j + 1) * COL)
                dz[l][slot, :, cols] = part.astype(BF16)
                db_acc[l, :, cols] += jnp.sum(part.reshape(ROWS // 8, 8, COL), axis=0)
        for k in range(KT):
            prod = sum_dots([(dz[l][slot, :, n * COL:(n + 1) * COL], w[l, k, n]) for n in range(NT)])
            if k >= KT // 2:
                dr[l][:, (k - KT // 2) * COL:(k - KT // 2 + 1) * COL] = prod
            else:
                kc = slice(k * COL, (k + 1) * COL)
                total = (dy_buf[t, :, kc] if l == LOCAL - 1 else dyn[l][:, kc]) + prod
                if l > 0:
                    dyn[l - 1][:, kc] = total
                else:
                    dx_out[out_slot, :, kc] = total

    def bwd_wave(s, full):
        t_of = [STEPS + LOCAL - 2 - s - l for l in range(LOCAL)]
        slot_of = [lax.rem(t + RING, 2) for t in t_of]
        t_top, t_low = t_of[LOCAL - 1], t_of[0]
        out_slot = lax.rem(t_low + 2 * RING, RING)

        @pl.when(jnp.logical_and(second, both(valid(t_top, full), lax.rem(t_top, PIECE) == PIECE - 1)))
        def _():
            p = t_top // PIECE
            pltpu.make_async_copy(dy_buf.at[pl.ds(p * PIECE, PIECE)], dy_buf.at[pl.ds(p * PIECE, PIECE)], din_sem.at[p]).wait()

        @pl.when(both(valid(t_top, full), first))
        def _():
            dy_copy(t_top, 0).wait_recv()

        for l in range(LOCAL):
            t, slot = t_of[l], slot_of[l]

            @guard(True if full else jnp.logical_and(t >= 0, t < STEPS - 2))
            def _():
                rec_read(l, t, slot).wait()
                dz_write(l, t + 2, slot).wait()

        @pl.when(jnp.logical_and(t_low >= 0, t_low < STEPS - RING))
        def _():
            @pl.when(second)
            def _():
                dy_copy(t_low + RING, out_slot).wait_send()

            @pl.when(first)
            def _():
                home_copy(t_low + RING, out_slot).wait_send()
                own_copy(t_low + RING, out_slot).wait()

        for l in range(LOCAL):
            if full:
                bwd_cell(l, t_of[l], slot_of[l])
            else:
                @pl.when(valid(t_of[l], False))
                def _():
                    bwd_cell(l, t_of[l], slot_of[l])

        for l in range(LOCAL):
            t, slot = t_of[l], slot_of[l]

            @pl.when(both(valid(t, full), t >= 2))
            def _():
                rec_read(l, t - 2, slot).start()

            @guard(valid(t, full))
            def _():
                dz_write(l, t, slot).start()

        @pl.when(both(valid(t_low, full), second))
        def _():
            dy_copy(t_low, out_slot).start()

        @pl.when(both(valid(t_low, full), first))
        def _():
            home_copy(t_low, out_slot).start()
            own_copy(t_low, out_slot).start()

    run_waves(bwd_wave, 0, LOCAL + 1, False)
    run_waves(bwd_wave, LOCAL + 1, STEPS, True)
    run_waves(bwd_wave, STEPS, STEPS + LOCAL - 1, False)

    for l in range(LOCAL):
        db_sum[l:l + 1, :] = jnp.sum(db_acc[l], axis=0, keepdims=True)
    db_local = pltpu.make_async_copy(db_sum, db_hbm.at[core], db_sem.at[0])
    db_remote = pltpu.make_async_remote_copy(db_sum, db_hbm.at[core], db_sem.at[1], db_sem.at[2], device_id=partner, device_id_type=MESH)
    db_local.start()
    db_remote.start()

    for p in range(PIECES):
        gathered(x_piece, p, 0)
        gathered(d_piece, p, 1)
    for l in range(LOCAL):
        for slot in range(2):
            dz_write(l, slot, slot).wait()

    @pl.when(first)
    def _():
        for s in range(RING):
            y_copy(STEPS - RING + s, s).wait_send()
            home_copy(s, s).wait_send()
            own_copy(s, s).wait()

    @pl.when(second)
    def _():
        for s in range(RING):
            dy_copy(s, s).wait_send()
        for t in range(STEPS):
            home_copy(t, 0).wait_recv()

    db_local.wait()
    db_remote.wait()


def recurrence_entry(n_data, *refs):
    ins, outs, rest = refs[:4], refs[4:9], list(refs[9:])
    take = lambda count: [rest.pop(0) for _ in range(count)]
    w, x_buf, dy_buf = take(3)
    lhs, hn, xn, cs, rec = take(4), take(4), take(3), take(4), take(4)
    y_out, = take(1)
    dz, dyn, dr, dc = take(4), take(3), take(4), take(4)
    dx_out, db_acc, db_sum = take(3)
    recurrence_kernel(n_data, *ins, *outs, w, x_buf, dy_buf, lhs, hn, xn, cs, rec, y_out, dz, dyn, dr, dc, dx_out, db_acc, db_sum, *rest)


def weight_kernel(n_data, xh, dz, dw_hbm, stage, local_sem, send_sem, recv_sem):
    rep, data = lax.axis_index('rep'), lax.axis_index('data')
    core = lax.rem(data, 2)
    partner = {'rep': rep, 'data': data + 1 - 2 * core}
    i = pl.program_id(0)
    total = LOCAL * NT
    slot = lax.rem(i, 2)

    def out(step):
        return dw_hbm.at[core * LOCAL + step // NT, :, pl.ds(pl.multiple_of(lax.rem(step, NT) * COL, COL), COL)]

    def near(step, slot):
        return pltpu.make_async_copy(stage.at[slot], out(step), local_sem.at[slot])

    def far(step, slot):
        return pltpu.make_async_remote_copy(stage.at[slot], out(step), send_sem.at[slot], recv_sem.at[step], device_id=partner, device_id_type=MESH)

    @pl.when(i >= 2)
    def _():
        near(i - 2, slot).wait()
        far(i - 2, slot).wait_send()

    stage[slot] = lax.dot_general(xh[0], dz[0], (((0,), (0,)), ((), ())), preferred_element_type=F32)
    near(i, slot).start()
    far(i, slot).start()

    @pl.when(i == total - 1)
    def _():
        for back in range(2):
            near(total - 2 + back, back).wait()
            far(total - 2 + back, back).wait_send()
        for step in range(total):
            far(step, 0).wait_recv()


def solution(mesh):
    batch_axes = tuple(mesh.axis_names)
    n_data = mesh.shape['data']
    hbm = pl.BlockSpec(memory_space=pl.ANY)
    dma = pltpu.SemaphoreType.DMA

    def device_step(x_in, d_out, weights, biases):
        x_seq = jnp.swapaxes(x_in, 0, 1)
        d_seq = jnp.swapaxes(d_out, 0, 1)
        plane = lambda dtype: pltpu.VMEM((ROWS, HID), dtype)
        xh, dz, dx, db, _ = pl.pallas_call(
            functools.partial(recurrence_entry, n_data),
            out_shape=(jax.ShapeDtypeStruct((LOCAL, STEPS, ROWS, 2 * HID), BF16),
                       jax.ShapeDtypeStruct((LOCAL, STEPS, ROWS, GATES), BF16),
                       jax.ShapeDtypeStruct((STEPS, OWN, HID), F32),
                       jax.ShapeDtypeStruct((2, LOCAL, GATES), F32),
                       jax.ShapeDtypeStruct((LOCAL, STEPS, ROWS, REC), F32)),
            in_specs=[hbm, hbm, hbm, pl.BlockSpec(memory_space=pltpu.VMEM)],
            out_specs=(hbm,) * 5,
            scratch_shapes=[
                pltpu.VMEM((LOCAL, KT, NT, COL, COL), BF16),
                pltpu.VMEM((STEPS, ROWS, HID), BF16),
                pltpu.VMEM((STEPS, ROWS, HID), F32),
                *[pltpu.VMEM((2, ROWS, 2 * HID), BF16)] * 4,
                *[plane(BF16)] * 4,
                *[plane(BF16)] * 3,
                *[plane(F32)] * 4,
                *[pltpu.VMEM((2, ROWS, REC), F32)] * 4,
                pltpu.VMEM((RING, ROWS, HID), BF16),
                *[pltpu.VMEM((2, ROWS, GATES), BF16)] * 4,
                *[plane(F32)] * 3,
                *[plane(F32)] * 4,
                *[plane(F32)] * 4,
                pltpu.VMEM((RING, ROWS, HID), F32),
                pltpu.VMEM((LOCAL, 8, GATES), F32),
                pltpu.VMEM((LOCAL, GATES), F32),
                dma((LOCAL,)), dma((STEPS,)), dma((PIECES,)), dma((PIECES, CHIPS)), dma((RING,)), dma((LOCAL, 2)), dma((LOCAL, 2)), dma((LOCAL, 2)),
                dma((STEPS,)), dma((PIECES,)), dma((PIECES, CHIPS)), dma((LOCAL, 2)), dma((RING,)), dma((RING,)), dma((STEPS,)), dma((3,)),
            ],
            compiler_params=pltpu.CompilerParams(has_side_effects=True, vmem_limit_bytes=66000000),
        )(x_seq, d_seq, weights, biases)
        dw = pl.pallas_call(
            functools.partial(weight_kernel, n_data),
            out_shape=jax.ShapeDtypeStruct((2 * LOCAL, 2 * HID, GATES), F32),
            grid=(LOCAL * NT,),
            in_specs=[pl.BlockSpec((1, STEPS * ROWS, 2 * HID), lambda i: (i // NT, 0, 0)),
                      pl.BlockSpec((1, STEPS * ROWS, COL), lambda i: (i // NT, 0, lax.rem(i, NT)))],
            out_specs=hbm,
            scratch_shapes=[pltpu.VMEM((2, 2 * HID, COL), F32), dma((2,)), dma((2,)), dma((LOCAL * NT,))],
            compiler_params=pltpu.CompilerParams(has_side_effects=True, vmem_limit_bytes=60000000),
        )(xh.reshape(LOCAL, STEPS * ROWS, 2 * HID), dz.reshape(LOCAL, STEPS * ROWS, GATES))
        return dw, db.reshape(2 * LOCAL, GATES), jnp.swapaxes(dx, 0, 1)

    return jax.shard_map(device_step, mesh=mesh,
                         in_specs=(P(batch_axes), P(batch_axes), P(), P()),
                         out_specs=(P(), P(), P(batch_axes)), check_vma=False)
```

time: 3550 us -> 378 us (0.11); the launches traced: 3490 us -> 378 us
  matrix products: 1310 us -> 0 us
  other arithmetic: 999 us -> 0 us
  waiting for transfers between devices: 740 us -> 0 us
  local copies, waits for them, and re-layouts: 415 us -> 51.1 us
  Pallas kernels: 0 us -> 326 us
    dot_general x544 -> x0, matrix products: 1310 us -> none  [the longest x256 653 us: time_step(): z_all = z_in + jnp.dot(h_prev, w_rec, preferred_element_type=jnp.float32)]
    psum x2 -> x0, waiting for transfers between devices: 740 us -> none  [the longest x1 740 us: device_step(): dw_parts.insert(0, lax.psum(dw_layer, batch_axes))]
    dynamic_update_slice x992 -> x0, other arithmetic: 494 us -> none  [the longest x736 332 us: layer_forward(): lax.scan(time_step, init_state, (x_proj, x_seq))]
    concatenate x512 -> x0, other arithmetic: 448 us -> none  [time_step(): jnp.concatenate([dc_tot * cand_g * in_g * (1.0 - in_g), dc_tot * c_prev *...]
    pallas_call x0 -> x2, Pallas kernels: none -> 326 us  [the longest x1 231 us: device_step(): pl.pallas_call(functools.partial(recurrence_entry, n_data), out_shape=(ja...]
    squeeze x256 -> x0, local copies, waits for them, and re-layouts: 234 us -> none  [layer_forward(): lax.scan(time_step, init_state, (x_proj, x_seq))]
    another operation x57 -> x0, local copies, waits for them, and re-layouts: 57.2 us -> none
    dynamic_update_slice x256 -> x0, local copies, waits for them, and re-layouts: 47.6 us -> none  [layer_backward(): lax.scan(time_step, (zero_state, zero_state), (dy_seq, z_seq, c_prev_seq)...]
  transfers between devices with their start and end apart: 2 -> 0, of which waited for: 1 -> 0; matrix products, arithmetic and copies ran while one was open for 3% -> 0% of each run, Pallas kernels for 0% -> 0%
where the time goes in v2:
time: 378 us
  Pallas kernels  326 us (86%)
  local copies, waits for them, and re-layouts  51.1 us (14%)
    pallas_call x1, Pallas kernels, device_step(): pl.pallas_call(functools.partial(recurrence_entry, n_data), out_shape=(ja...  231 us
    pallas_call x1, Pallas kernels, device_step(): pl.pallas_call(functools.partial(weight_kernel, n_data), out_shape=jax.Sh...  95.1 us
    unnamed x8, local copies, waits for them, and re-layouts  50.4 us

profile of v2, /device:TPU:0, one launch (start us, length us, event | category | flops | bytes accessed | tf_op | source)
XLA Modules:
  0.0 377.8 jit_solution(17524213860804928472)
XLA Ops:
  0.6 2.1 copy.13
  2.8 2.8 copy.12
  5.6 231.0 %shard_map.67 = (bf16[4,32,128,1024]{3,2,1,0:T(8,128)(2,1)}, bf16[4,32,128,2048]{3,2,1,0:T(8,128)(2,1)}, f32[32,16,512]{2,1,0:T(8,128)}, f32[2,4,2048]{2,1,0:T(4,128)}, f32[4,32,128,2560]{3,2,1,0:T(8,128)}) custom-call(bf16[32,16,512]{2,1,0:T(8,128)(2,1)} %bitcast.11, f32[32,16,512]{2,1,0:T(8,128)} %bitcast.10, bf16[8,1024,2048]{2,1,0:T(8,128)(2,1)} %refs_2_.1, ...), custom_call_target="tpu_custom_call" | custom-call | tf_op jit(solution)/shard_map/pallas_call | solution.py:434
  236.6 0.0 copy-start.1
  236.6 0.0 copy-start
  236.6 95.1 %shard_map.68 = f32[8,1024,2048]{2,1,0:T(8,128)} custom-call(bf16[4,4096,1024]{2,1,0:T(8,128)(2,1)} %bitcast.9, bf16[4,4096,2048]{2,1,0:T(8,128)(2,1)} %bitcast.3.dz), custom_call_target="tpu_custom_call" | custom-call | tf_op jit(solution)/shard_map/pallas_call | solution.py:465
  331.7 0.0 copy-done.1
  331.7 0.7 reshape.17
  332.3 0.0 copy-done
  332.3 1.6 copy.9
  333.9 43.9 %copy.15 = f32[8,1024,2048]{2,1,0:T(8,128)} copy(f32[8,1024,2048]{2,1,0:T(8,128)} %shard_map.68) | data formatting | bytes 134217728
Async XLA Ops:
  236.6 95.1 %copy-start.1 = (f32[2,4,2048]{2,1,0:T(4,128)S(1)}, f32[2,4,2048]{2,1,0:T(4,128)}, u32[]{:S(2)}) copy-start(f32[2,4,2048]{2,1,0:T(4,128)} %get-tuple-element.9) | copy-start | bytes 196612
  236.6 95.7 %copy-start = (f32[32,16,512]{2,1,0:T(8,128)S(1)}, f32[32,16,512]{2,1,0:T(8,128)}, u32[]{:S(2)}) copy-start(f32[32,16,512]{2,1,0:T(8,128)} %get-tuple-element.10) | copy-start | bytes 3145732

commit v3 on v2

--- a/solution.py
+++ b/solution.py
@@ -21,6 +21,7 @@
 NT = GATES // COL
 REC = 5 * HID
 RING = 4
+SLOTS = 3
 F32 = jnp.float32
 BF16 = jnp.bfloat16
 MESH = pl.DeviceIdType.MESH
@@ -146,7 +147,7 @@
 
     def fwd_wave(s, full):
         t_of = [s - l for l in range(LOCAL)]
-        slot_of = [lax.rem(t + RING, 2) for t in t_of]
+        slot_of = [lax.rem(t + SLOTS, SLOTS) for t in t_of]
 
         @pl.when(jnp.logical_and(first, both(valid(s, full), lax.rem(s, PIECE) == 0)))
         def _():
@@ -160,10 +161,10 @@
         for l in range(LOCAL):
             t, slot = t_of[l], slot_of[l]
 
-            @guard(True if full else jnp.logical_and(t >= 2, t < STEPS))
-            def _():
-                lhs_write(l, t - 2, slot).wait()
-                rec_write(l, t - 2, slot).wait()
+            @guard(True if full else jnp.logical_and(t >= SLOTS, t < STEPS))
+            def _():
+                lhs_write(l, t - SLOTS, slot).wait()
+                rec_write(l, t - SLOTS, slot).wait()
 
         t_top = t_of[LOCAL - 1]
 
@@ -194,7 +195,7 @@
             def _():
                 lhs_write(l, t, slot).start()
 
-            @pl.when(both(valid(t, full), t < STEPS - 2))
+            @pl.when(both(valid(t, full), t < STEPS - SLOTS))
             def _():
                 rec_write(l, t, slot).start()
 
@@ -208,8 +209,8 @@
             return carry
         lax.fori_loop(lo, hi, body, 0)
 
-    run_waves(fwd_wave, 0, LOCAL + 1, False)
-    run_waves(fwd_wave, LOCAL + 1, STEPS, True)
+    run_waves(fwd_wave, 0, LOCAL - 1 + SLOTS, False)
+    run_waves(fwd_wave, LOCAL - 1 + SLOTS, STEPS, True)
     run_waves(fwd_wave, STEPS, STEPS + LOCAL - 1, False)
 
     def turn(i, carry):
@@ -223,8 +224,8 @@
     lax.fori_loop(0, KT * NT, turn, 0)
 
     for l in range(LOCAL):
-        for slot in range(2):
-            lhs_write(l, STEPS - 2 + slot, slot).wait()
+        for t in range(STEPS - SLOTS, STEPS):
+            lhs_write(l, t, t % SLOTS).wait()
 
     def rec_read(l, t, slot):
         return pltpu.make_async_copy(rec_hbm.at[l, t], rec[l].at[slot], rec_rsem.at[l, slot])
@@ -279,7 +280,7 @@
 
     def bwd_wave(s, full):
         t_of = [STEPS + LOCAL - 2 - s - l for l in range(LOCAL)]
-        slot_of = [lax.rem(t + RING, 2) for t in t_of]
+        slot_of = [lax.rem(t + SLOTS, SLOTS) for t in t_of]
         t_top, t_low = t_of[LOCAL - 1], t_of[0]
         out_slot = lax.rem(t_low + 2 * RING, RING)
 
@@ -295,10 +296,10 @@
         for l in range(LOCAL):
             t, slot = t_of[l], slot_of[l]
 
-            @guard(True if full else jnp.logical_and(t >= 0, t < STEPS - 2))
+            @guard(True if full else jnp.logical_and(t >= 0, t < STEPS - SLOTS))
             def _():
                 rec_read(l, t, slot).wait()
-                dz_write(l, t + 2, slot).wait()
+                dz_write(l, t + SLOTS, slot).wait()
 
         @pl.when(jnp.logical_and(t_low >= 0, t_low < STEPS - RING))
         def _():
@@ -322,9 +323,9 @@
         for l in range(LOCAL):
             t, slot = t_of[l], slot_of[l]
 
-            @pl.when(both(valid(t, full), t >= 2))
-            def _():
-                rec_read(l, t - 2, slot).start()
+            @pl.when(both(valid(t, full), t >= SLOTS))
+            def _():
+                rec_read(l, t - SLOTS, slot).start()
 
             @guard(valid(t, full))
             def _():
@@ -339,8 +340,8 @@
             home_copy(t_low, out_slot).start()
             own_copy(t_low, out_slot).start()
 
-    run_waves(bwd_wave, 0, LOCAL + 1, False)
-    run_waves(bwd_wave, LOCAL + 1, STEPS, True)
+    run_waves(bwd_wave, 0, LOCAL - 1 + SLOTS, False)
+    run_waves(bwd_wave, LOCAL - 1 + SLOTS, STEPS, True)
     run_waves(bwd_wave, STEPS, STEPS + LOCAL - 1, False)
 
     for l in range(LOCAL):
@@ -354,8 +355,8 @@
         gathered(x_piece, p, 0)
         gathered(d_piece, p, 1)
     for l in range(LOCAL):
-        for slot in range(2):
-            dz_write(l, slot, slot).wait()
+        for t in range(SLOTS):
+            dz_write(l, t, t).wait()
 
     @pl.when(first)
     def _():
@@ -386,7 +387,7 @@
     recurrence_kernel(n_data, *ins, *outs, w, x_buf, dy_buf, lhs, hn, xn, cs, rec, y_out, dz, dyn, dr, dc, dx_out, db_acc, db_sum, *rest)
 
 
-def weight_kernel(n_data, xh, dz, dw_hbm, stage, local_sem, send_sem, recv_sem):
+def weight_kernel(n_data, xh_hbm, dz, dw_hbm, xh, stage, xh_sem, local_sem, send_sem, recv_sem):
     rep, data = lax.axis_index('rep'), lax.axis_index('data')
     core = lax.rem(data, 2)
     partner = {'rep': rep, 'data': data + 1 - 2 * core}
@@ -403,12 +404,33 @@
     def far(step, slot):
         return pltpu.make_async_remote_copy(stage.at[slot], out(step), send_sem.at[slot], recv_sem.at[step], device_id=partner, device_id_type=MESH)
 
+    layer, n = i // NT, lax.rem(i, NT)
+    part = STEPS * ROWS // NT
+
+    def load(layer, p):
+        rows = pl.ds(pl.multiple_of(p * part, part), part)
+        return pltpu.make_async_copy(xh_hbm.at[layer, rows], xh.at[lax.rem(layer, 2), rows], xh_sem.at[lax.rem(layer, 2), p])
+
+    @pl.when(i == 0)
+    def _():
+        for p in range(NT):
+            load(0, p).start()
+
+    @pl.when(n == 0)
+    def _():
+        for p in range(NT):
+            load(layer, p).wait()
+
+    @pl.when(layer + 1 < LOCAL)
+    def _():
+        load(layer + 1, n).start()
+
     @pl.when(i >= 2)
     def _():
         near(i - 2, slot).wait()
         far(i - 2, slot).wait_send()
 
-    stage[slot] = lax.dot_general(xh[0], dz[0], (((0,), (0,)), ((), ())), preferred_element_type=F32)
+    stage[slot] = lax.dot_general(xh[lax.rem(layer, 2)], dz[0], (((0,), (0,)), ((), ())), preferred_element_type=F32)
     near(i, slot).start()
     far(i, slot).start()
 
@@ -444,21 +466,21 @@
                 pltpu.VMEM((LOCAL, KT, NT, COL, COL), BF16),
                 pltpu.VMEM((STEPS, ROWS, HID), BF16),
                 pltpu.VMEM((STEPS, ROWS, HID), F32),
-                *[pltpu.VMEM((2, ROWS, 2 * HID), BF16)] * 4,
+                *[pltpu.VMEM((SLOTS, ROWS, 2 * HID), BF16)] * 4,
                 *[plane(BF16)] * 4,
                 *[plane(BF16)] * 3,
                 *[plane(F32)] * 4,
-                *[pltpu.VMEM((2, ROWS, REC), F32)] * 4,
+                *[pltpu.VMEM((SLOTS, ROWS, REC), F32)] * 4,
                 pltpu.VMEM((RING, ROWS, HID), BF16),
-                *[pltpu.VMEM((2, ROWS, GATES), BF16)] * 4,
+                *[pltpu.VMEM((SLOTS, ROWS, GATES), BF16)] * 4,
                 *[plane(F32)] * 3,
                 *[plane(F32)] * 4,
                 *[plane(F32)] * 4,
                 pltpu.VMEM((RING, ROWS, HID), F32),
                 pltpu.VMEM((LOCAL, 8, GATES), F32),
                 pltpu.VMEM((LOCAL, GATES), F32),
-                dma((LOCAL,)), dma((STEPS,)), dma((PIECES,)), dma((PIECES, CHIPS)), dma((RING,)), dma((LOCAL, 2)), dma((LOCAL, 2)), dma((LOCAL, 2)),
-                dma((STEPS,)), dma((PIECES,)), dma((PIECES, CHIPS)), dma((LOCAL, 2)), dma((RING,)), dma((RING,)), dma((STEPS,)), dma((3,)),
+                dma((LOCAL,)), dma((STEPS,)), dma((PIECES,)), dma((PIECES, CHIPS)), dma((RING,)), dma((LOCAL, SLOTS)), dma((LOCAL, SLOTS)), dma((LOCAL, SLOTS)),
+                dma((STEPS,)), dma((PIECES,)), dma((PIECES, CHIPS)), dma((LOCAL, SLOTS)), dma((RING,)), dma((RING,)), dma((STEPS,)), dma((3,)),
             ],
             compiler_params=pltpu.CompilerParams(has_side_effects=True, vmem_limit_bytes=66000000),
         )(x_seq, d_seq, weights, biases)
@@ -466,10 +488,10 @@
             functools.partial(weight_kernel, n_data),
             out_shape=jax.ShapeDtypeStruct((2 * LOCAL, 2 * HID, GATES), F32),
             grid=(LOCAL * NT,),
-            in_specs=[pl.BlockSpec((1, STEPS * ROWS, 2 * HID), lambda i: (i // NT, 0, 0)),
+            in_specs=[hbm,
                       pl.BlockSpec((1, STEPS * ROWS, COL), lambda i: (i // NT, 0, lax.rem(i, NT)))],
             out_specs=hbm,
-            scratch_shapes=[pltpu.VMEM((2, 2 * HID, COL), F32), dma((2,)), dma((2,)), dma((LOCAL * NT,))],
+            scratch_shapes=[pltpu.VMEM((2, STEPS * ROWS, 2 * HID), BF16), pltpu.VMEM((2, 2 * HID, COL), F32), dma((2, NT)), dma((2,)), dma((2,)), dma((LOCAL * NT,))],
             compiler_params=pltpu.CompilerParams(has_side_effects=True, vmem_limit_bytes=60000000),
         )(xh.reshape(LOCAL, STEPS * ROWS, 2 * HID), dz.reshape(LOCAL, STEPS * ROWS, GATES))
         return dw, db.reshape(2 * LOCAL, GATES), jnp.swapaxes(dx, 0, 1)

time: 378 us -> 376 us (level)
    pallas_call x1, Pallas kernels: 95.1 us -> 90.7 us  [device_step(): pl.pallas_call(functools.partial(weight_kernel, n_data), out_shape=jax.Sh...]
where the time goes in v3:
time: 376 us; the launch traced here: 375 us
  Pallas kernels  324 us (86%)
  local copies, waits for them, and re-layouts  51.1 us (14%)
    pallas_call x1, Pallas kernels, device_step(): pl.pallas_call(functools.partial(recurrence_entry, n_data), out_shape=(ja...  233 us
    pallas_call x1, Pallas kernels, device_step(): pl.pallas_call(functools.partial(weight_kernel, n_data), out_shape=jax.Sh...  90.7 us
    unnamed x8, local copies, waits for them, and re-layouts  50.4 us

profile of v3, /device:TPU:0, one launch (start us, length us, event | category | flops | bytes accessed | tf_op | source)
XLA Modules:
  0.0 375.4 jit_solution(12754638062343343502)
XLA Ops:
  0.6 2.1 copy.13
  2.8 2.8 copy.12
  5.6 233.0 %shard_map.67 = (bf16[4,32,128,1024]{3,2,1,0:T(8,128)(2,1)}, bf16[4,32,128,2048]{3,2,1,0:T(8,128)(2,1)}, f32[32,16,512]{2,1,0:T(8,128)}, f32[2,4,2048]{2,1,0:T(4,128)}, f32[4,32,128,2560]{3,2,1,0:T(8,128)}) custom-call(bf16[32,16,512]{2,1,0:T(8,128)(2,1)} %bitcast.11, f32[32,16,512]{2,1,0:T(8,128)} %bitcast.10, bf16[8,1024,2048]{2,1,0:T(8,128)(2,1)} %refs_2_.1, ...), custom_call_target="tpu_custom_call" | custom-call | tf_op jit(solution)/shard_map/pallas_call | solution.py:456
  238.5 0.0 copy-start.1
  238.5 0.0 copy-start
  238.6 90.7 %shard_map.68 = f32[8,1024,2048]{2,1,0:T(8,128)} custom-call(bf16[4,4096,1024]{2,1,0:T(8,128)(2,1)} %bitcast.9, bf16[4,4096,2048]{2,1,0:T(8,128)(2,1)} %bitcast.3.dz), custom_call_target="tpu_custom_call" | custom-call | tf_op jit(solution)/shard_map/pallas_call | solution.py:487
  329.2 0.0 copy-done.1
  329.2 0.7 reshape.17
  329.9 0.0 copy-done
  329.9 1.6 copy.9
  331.5 43.9 %copy.15 = f32[8,1024,2048]{2,1,0:T(8,128)} copy(f32[8,1024,2048]{2,1,0:T(8,128)} %shard_map.68) | data formatting | bytes 134217728
Async XLA Ops:
  238.5 90.7 %copy-start.1 = (f32[2,4,2048]{2,1,0:T(4,128)S(1)}, f32[2,4,2048]{2,1,0:T(4,128)}, u32[]{:S(2)}) copy-start(f32[2,4,2048]{2,1,0:T(4,128)} %get-tuple-element.9) | copy-start | bytes 196612
  238.5 91.4 %copy-start = (f32[32,16,512]{2,1,0:T(8,128)S(1)}, f32[32,16,512]{2,1,0:T(8,128)}, u32[]{:S(2)}) copy-start(f32[32,16,512]{2,1,0:T(8,128)} %get-tuple-element.10) | copy-start | bytes 3145732

commit v4 on v3

--- a/solution.py
+++ b/solution.py
@@ -21,7 +21,7 @@
 NT = GATES // COL
 REC = 5 * HID
 RING = 4
-SLOTS = 3
+SLOTS = 2
 F32 = jnp.float32
 BF16 = jnp.bfloat16
 MESH = pl.DeviceIdType.MESH
@@ -56,7 +56,7 @@
         return {'rep': dev // n_data, 'data': dev % n_data}
 
     def w_copy(l, k, n):
-        return pltpu.make_async_copy(w_hbm.at[core * LOCAL + l, pl.ds(k * COL, COL), pl.ds(n * COL, COL)], w.at[l, k, n], w_sem.at[l])
+        return pltpu.make_async_copy(w_hbm.at[core * LOCAL + l, pl.ds(k * COL, COL), pl.ds(n * COL, COL)], w[l].at[k, n], w_sem.at[l])
 
     def x_piece(p, dev, remote):
         src, dst = x_hbm.at[pl.ds(p * PIECE, PIECE)], x_buf.at[pl.ds(p * PIECE, PIECE), my_rows]
@@ -86,22 +86,17 @@
             def _():
                 piece(p, dev, True).wait_send()
 
-    for p in range(PIECES):
-        gather(x_piece, p, 0)
+    gather(x_piece, 0, 0)
     for l in range(LOCAL):
         for k in range(KT):
             for n in range(NT):
                 w_copy(l, k, n).start()
-    for p in reversed(range(PIECES)):
-        gather(d_piece, p, 1)
+        if l == 0:
+            gather(x_piece, 1, 0)
 
     for l in range(LOCAL):
         hn[l][...] = jnp.zeros((ROWS, HID), BF16)
         cs[l][...] = jnp.zeros((ROWS, HID), F32)
-    for l in range(LOCAL):
-        for k in range(KT):
-            for n in range(NT):
-                w_copy(l, k, n).wait()
 
     def y_copy(t, slot):
         return pltpu.make_async_remote_copy(y_out.at[slot], x_buf.at[t], y_send.at[slot], x_sem.at[t], device_id=partner, device_id_type=MESH)
@@ -129,7 +124,7 @@
             z = []
             for q in range(4):
                 n = q * (HID // COL) + j
-                z.append(sum_dots([(lhs[l][slot, :, k * COL:(k + 1) * COL], w[l, k, n]) for k in range(KT)])
+                z.append(sum_dots([(lhs[l][slot, :, k * COL:(k + 1) * COL], w[l][k, n]) for k in range(KT)])
                          + bias[pl.ds(core * LOCAL + l, 1), n * COL:(n + 1) * COL])
             in_g, fg_g, cand_g, out_g = jax.nn.sigmoid(z[0]), jax.nn.sigmoid(z[1]), jnp.tanh(z[2]), jax.nn.sigmoid(z[3])
             c_prev = cs[l][:, hc]
@@ -158,10 +153,16 @@
         def _():
             y_copy(s, 0).wait_recv()
 
+        if not full:
+            for l in range(LOCAL):
+                @pl.when(s == l)
+                def _():
+                    pltpu.make_async_copy(w[l], w[l], w_sem.at[l]).wait()
+
         for l in range(LOCAL):
             t, slot = t_of[l], slot_of[l]
 
-            @guard(True if full else jnp.logical_and(t >= SLOTS, t < STEPS))
+            @pl.when(jnp.logical_and(t >= SLOTS, t < STEPS))
             def _():
                 lhs_write(l, t - SLOTS, slot).wait()
                 rec_write(l, t - SLOTS, slot).wait()
@@ -203,25 +204,35 @@
         def _():
             y_copy(t_top, lax.rem(t_top, RING)).start()
 
+        turn_of = s // 2
+
+        @pl.when(jnp.logical_and(lax.rem(s, 2) == 0, turn_of < PIECES - 2))
+        def _():
+            gather(x_piece, turn_of + 2, 0)
+
+        @pl.when(jnp.logical_and(lax.rem(s, 2) == 0, jnp.logical_and(turn_of >= PIECES - 2, turn_of < 2 * PIECES - 2)))
+        def _():
+            gather(d_piece, 2 * PIECES - 3 - turn_of, 1)
+
     def run_waves(wave, lo, hi, full):
         def body(s, carry):
             wave(s, full)
             return carry
         lax.fori_loop(lo, hi, body, 0)
 
-    run_waves(fwd_wave, 0, LOCAL - 1 + SLOTS, False)
-    run_waves(fwd_wave, LOCAL - 1 + SLOTS, STEPS, True)
+    run_waves(fwd_wave, 0, LOCAL, False)
+    run_waves(fwd_wave, LOCAL, STEPS, True)
     run_waves(fwd_wave, STEPS, STEPS + LOCAL - 1, False)
 
     def turn(i, carry):
-        k, n = i // NT, lax.rem(i, NT)
-        for l0 in range(0, LOCAL, 2):
-            tiles = [w[l, k, n].T for l in (l0, l0 + 1)]
-            for l, tile in zip((l0, l0 + 1), tiles):
-                w[l, k, n] = tile
+        k, n = i // (NT // 2), 2 * lax.rem(i, NT // 2)
+        for l in range(LOCAL):
+            left, right = w[l][k, n].T, w[l][k, n + 1].T
+            w[l][k, n] = left
+            w[l][k, n + 1] = right
         return carry
 
-    lax.fori_loop(0, KT * NT, turn, 0)
+    lax.fori_loop(0, KT * NT // 2, turn, 0)
 
     for l in range(LOCAL):
         for t in range(STEPS - SLOTS, STEPS):
@@ -267,7 +278,7 @@
                 dz[l][slot, :, cols] = part.astype(BF16)
                 db_acc[l, :, cols] += jnp.sum(part.reshape(ROWS // 8, 8, COL), axis=0)
         for k in range(KT):
-            prod = sum_dots([(dz[l][slot, :, n * COL:(n + 1) * COL], w[l, k, n]) for n in range(NT)])
+            prod = sum_dots([(dz[l][slot, :, n * COL:(n + 1) * COL], w[l][k, n]) for n in range(NT)])
             if k >= KT // 2:
                 dr[l][:, (k - KT // 2) * COL:(k - KT // 2 + 1) * COL] = prod
             else:
@@ -296,7 +307,7 @@
         for l in range(LOCAL):
             t, slot = t_of[l], slot_of[l]
 
-            @guard(True if full else jnp.logical_and(t >= 0, t < STEPS - SLOTS))
+            @pl.when(jnp.logical_and(t >= 0, t < STEPS - SLOTS))
             def _():
                 rec_read(l, t, slot).wait()
                 dz_write(l, t + SLOTS, slot).wait()
@@ -340,8 +351,8 @@
             home_copy(t_low, out_slot).start()
             own_copy(t_low, out_slot).start()
 
-    run_waves(bwd_wave, 0, LOCAL - 1 + SLOTS, False)
-    run_waves(bwd_wave, LOCAL - 1 + SLOTS, STEPS, True)
+    run_waves(bwd_wave, 0, LOCAL - 1, False)
+    run_waves(bwd_wave, LOCAL - 1, STEPS, True)
     run_waves(bwd_wave, STEPS, STEPS + LOCAL - 1, False)
 
     for l in range(LOCAL):
@@ -379,7 +390,8 @@
 def recurrence_entry(n_data, *refs):
     ins, outs, rest = refs[:4], refs[4:9], list(refs[9:])
     take = lambda count: [rest.pop(0) for _ in range(count)]
-    w, x_buf, dy_buf = take(3)
+    w = take(4)
+    x_buf, dy_buf = take(2)
     lhs, hn, xn, cs, rec = take(4), take(4), take(3), take(4), take(4)
     y_out, = take(1)
     dz, dyn, dr, dc = take(4), take(3), take(4), take(4)
@@ -463,7 +475,7 @@
             in_specs=[hbm, hbm, hbm, pl.BlockSpec(memory_space=pltpu.VMEM)],
             out_specs=(hbm,) * 5,
             scratch_shapes=[
-                pltpu.VMEM((LOCAL, KT, NT, COL, COL), BF16),
+                *[pltpu.VMEM((KT, NT, COL, COL), BF16)] * 4,
                 pltpu.VMEM((STEPS, ROWS, HID), BF16),
                 pltpu.VMEM((STEPS, ROWS, HID), F32),
                 *[pltpu.VMEM((SLOTS, ROWS, 2 * HID), BF16)] * 4,

time: 376 us -> 369 us (0.981)
  Pallas kernels: 324 us -> 317 us
    pallas_call x1, Pallas kernels: 233 us -> 227 us  [device_step(): pl.pallas_call(functools.partial(recurrence_entry, n_data), out_shape=(ja...]
where the time goes in v4:
time: 369 us; the launch traced here: 368 us
  Pallas kernels  317 us (86%)
  local copies, waits for them, and re-layouts  51.1 us (14%)
    pallas_call x1, Pallas kernels, device_step(): pl.pallas_call(functools.partial(recurrence_entry, n_data), out_shape=(ja...  227 us
    pallas_call x1, Pallas kernels, device_step(): pl.pallas_call(functools.partial(weight_kernel, n_data), out_shape=jax.Sh...  89.5 us
    unnamed x8, local copies, waits for them, and re-layouts  50.4 us

profile of v4, /device:TPU:0, one launch (start us, length us, event | category | flops | bytes accessed | tf_op | source)
XLA Modules:
  0.0 368.3 jit_solution(3842285597509383332)
XLA Ops:
  0.6 2.1 copy.13
  2.8 2.8 copy.12
  5.6 227.0 %shard_map.67 = (bf16[4,32,128,1024]{3,2,1,0:T(8,128)(2,1)}, bf16[4,32,128,2048]{3,2,1,0:T(8,128)(2,1)}, f32[32,16,512]{2,1,0:T(8,128)}, f32[2,4,2048]{2,1,0:T(4,128)}, f32[4,32,128,2560]{3,2,1,0:T(8,128)}) custom-call(bf16[32,16,512]{2,1,0:T(8,128)(2,1)} %bitcast.11, f32[32,16,512]{2,1,0:T(8,128)} %bitcast.10, bf16[8,1024,2048]{2,1,0:T(8,128)(2,1)} %refs_2_.1, ...), custom_call_target="tpu_custom_call" | custom-call | tf_op jit(solution)/shard_map/pallas_call | solution.py:468
  232.5 0.0 copy-start.1
  232.6 0.0 copy-start
  232.6 89.5 %shard_map.68 = f32[8,1024,2048]{2,1,0:T(8,128)} custom-call(bf16[4,4096,1024]{2,1,0:T(8,128)(2,1)} %bitcast.9, bf16[4,4096,2048]{2,1,0:T(8,128)(2,1)} %bitcast.3.dz), custom_call_target="tpu_custom_call" | custom-call | tf_op jit(solution)/shard_map/pallas_call | solution.py:499
  322.1 0.0 copy-done.1
  322.1 0.7 reshape.17
  322.8 0.0 copy-done
  322.8 1.6 copy.9
  324.3 43.9 %copy.15 = f32[8,1024,2048]{2,1,0:T(8,128)} copy(f32[8,1024,2048]{2,1,0:T(8,128)} %shard_map.68) | data formatting | bytes 134217728
Async XLA Ops:
  232.5 89.6 %copy-start.1 = (f32[2,4,2048]{2,1,0:T(4,128)S(1)}, f32[2,4,2048]{2,1,0:T(4,128)}, u32[]{:S(2)}) copy-start(f32[2,4,2048]{2,1,0:T(4,128)} %get-tuple-element.9) | copy-start | bytes 196612
  232.6 90.2 %copy-start = (f32[32,16,512]{2,1,0:T(8,128)S(1)}, f32[32,16,512]{2,1,0:T(8,128)}, u32[]{:S(2)}) copy-start(f32[32,16,512]{2,1,0:T(8,128)} %get-tuple-element.10) | copy-start | bytes 3145732
